TPU v7x, 32 devices: a whole 2x2x4 slice. The times are simulated.
32 devices in a mesh: dp: 4 (over y, core), head: 2 (over x), kv: 4 (over z).
Axes of the slice: x: 2, y: 2, z: 4, core: 2. Of those that a mesh axis runs over, the one named last changes fastest.
Arguments:
- teacher_query: bfloat16 [4, 1024, 3584], P('dp', 'kv', 'head'), may hold values from -96 to 96
- teacher_key: bfloat16 [4, 1024, 512], P('dp', 'kv', 'head'), may hold values from -8 to 8
- student_query: bfloat16 [4, 1024, 1792], P('dp', 'kv', 'head'), may hold values from -96 to 96
- student_key: bfloat16 [4, 1024, 256], P('dp', 'kv', 'head'), may hold values from -8 to 8
- pair_table: int32 [14, 2], replicated, may hold values from 0 to 27, as said below
Outputs:
- kl: float32 [4, 14, 1024], P('dp', 'head', 'kv')
- head_loss: float32 [14], P('head')
Inputs may be any that keep to these rules, and one draw needn't show every extreme that they name: `pair_table`: each of the 28 teacher heads appears exactly once in the table.
All inputs are finite; a program needn't handle non-finite values.
Results may differ from a plain program's by a relative error of at most 0.0003.
Values may be sent and summed in bfloat16 or wider, within the bound.
A program may use at most 64 MiB of HBM per device.

v0:
```python
import math
import jax
import jax.numpy as jnp
from jax import lax
from jax.sharding import PartitionSpec as P

HT = 28
KVT = 4
DH = 128
HS = 14
KVS = 2
masked_value = -1e30


def running_softmax(running_max, running_total, logits, causal_mask):
    filled = jnp.where(causal_mask, logits, masked_value)
    new_max = jnp.maximum(running_max, jnp.max(filled, axis=-1))
    rescale = jnp.exp(running_max - new_max)
    weights = jnp.where(causal_mask, jnp.exp(filled - new_max[..., None]), 0.0)
    return (new_max, running_total * rescale + jnp.sum(weights, axis=-1), rescale, weights)


def make_fold(teacher_heads, teacher_select, student_heads, student_select, repeat, query_pos):
    seq_dev, row_count, pair_count, head_dim = teacher_heads.shape
    student_count = student_heads.shape[2]
    scale = 1.0 / math.sqrt(head_dim)
    last_query = query_pos[row_count - 1]

    def fold_step(carry, pieces, start):
        teacher_keys, student_keys = pieces
        key_count = teacher_keys.shape[1]
        block_size = math.gcd(key_count, 512)
        block_total = key_count // block_size
        visible = jnp.clip(last_query // block_size + 1, 0, block_total)

        def one_block(block_index, state):
            t_max, t_total, t_cross, s_max, s_total = state
            offset = block_index * block_size
            t_block = lax.dynamic_slice_in_dim(teacher_keys, offset, block_size, 1).reshape(
                seq_dev, block_size, -1, head_dim
            )
            s_block = lax.dynamic_slice_in_dim(student_keys, offset, block_size, 1).reshape(
                seq_dev, block_size, -1, head_dim
            )
            t_keys = jnp.take(t_block, teacher_select, axis=2)
            s_keys = jnp.take(s_block, student_select, axis=2)
            t_logits = (
                jnp.einsum(
                    "bqpd,bkpd->bpqk", teacher_heads, t_keys, preferred_element_type=jnp.float32
                )
                * scale
            )
            s_logits = (
                jnp.einsum(
                    "bqsd,bksd->bsqk", student_heads, s_keys, preferred_element_type=jnp.float32
                )
                * scale
            )
            key_pos = offset + jnp.arange(block_size, dtype=jnp.int32)
            causal_mask = key_pos[None, :] <= query_pos[:, None]
            t_max, t_total, t_rescale, t_weights = running_softmax(
                t_max, t_total, t_logits, causal_mask
            )
            s_max, s_total, s_rescale, s_weights = running_softmax(
                s_max, s_total, s_logits, causal_mask
            )
            split_logits = t_logits.reshape(seq_dev, student_count, repeat, row_count, block_size)
            gap = (split_logits - s_logits[:, :, None]).reshape(
                seq_dev, pair_count, row_count, block_size
            )
            t_cross = t_cross * t_rescale + jnp.sum(t_weights * gap, axis=-1)
            return (t_max, t_total, t_cross, s_max, s_total)

        return lax.fori_loop(0, visible, one_block, carry)

    pair_shape = (seq_dev, pair_count, row_count)
    student_shape = (seq_dev, student_count, row_count)
    initial = (
        jnp.full(pair_shape, masked_value, jnp.float32),
        jnp.zeros(pair_shape, jnp.float32),
        jnp.zeros(pair_shape, jnp.float32),
        jnp.full(student_shape, masked_value, jnp.float32),
        jnp.zeros(student_shape, jnp.float32),
    )
    return (fold_step, initial)


def finish_pairs(state, repeat):
    t_max, t_total, t_cross, s_max, s_total = state
    seq_dev, pair_count, row_count = t_max.shape
    student_count = s_max.shape[1]
    t_lse = t_max + jnp.log(t_total)
    s_lse = s_max + jnp.log(s_total)
    s_paired = jnp.broadcast_to(
        s_lse[:, :, None], (seq_dev, student_count, repeat, row_count)
    ).reshape(seq_dev, pair_count, row_count)
    return t_cross / t_total - t_lse + s_paired


def per_device(teacher_query, teacher_key, student_query, student_key, pair_table):
    seq_dev, row_count, teacher_width = teacher_query.shape
    n_head = lax.axis_size("head")
    n_kv = lax.axis_size("kv")
    n_data = lax.axis_size("dp")
    head_index = lax.axis_index("head")
    kv_index = lax.axis_index("kv")
    group_teacher = HT // KVT
    group_student = HS // KVS
    local_student = HS // n_head
    local_student_kv = KVS // n_head
    query_pos = kv_index * row_count + jnp.arange(row_count, dtype=jnp.int32)
    all_tq, all_tk = (
        lax.all_gather(teacher_query, "head", axis=2, tiled=True),
        lax.all_gather(teacher_key, "head", axis=2, tiled=True),
    )
    my_pairs = lax.dynamic_slice_in_dim(
        pair_table, head_index * local_student, local_student, 0
    ).reshape(-1)
    teacher_heads = jnp.take(all_tq.reshape(seq_dev, row_count, HT, DH), my_pairs, axis=2)
    teacher_select = my_pairs // group_teacher
    student_heads = student_query.reshape(seq_dev, row_count, local_student, DH)
    student_ids = head_index * local_student + jnp.arange(local_student, dtype=jnp.int32)
    student_select = student_ids // group_student - head_index * local_student_kv
    fold_step, initial = make_fold(
        teacher_heads, teacher_select, student_heads, student_select, 2, query_pos
    )
    state = fold_step(
        initial,
        (
            lax.all_gather(all_tk, "kv", axis=1, tiled=True),
            lax.all_gather(student_key, "kv", axis=1, tiled=True),
        ),
        jnp.int32(0),
    )
    pair_kl = finish_pairs(state, 2)
    kl_local = jnp.sum(pair_kl.reshape(seq_dev, local_student, 2, row_count), axis=2)
    head_sums = jnp.sum(kl_local, axis=(0, 2))
    total = lax.psum(head_sums, ("dp", "kv"))
    head_loss = total / (seq_dev * n_data * row_count * n_kv)
    return (kl_local, head_loss)


def solution(mesh):
    in_specs = (
        P("dp", "kv", "head"),
        P("dp", "kv", "head"),
        P("dp", "kv", "head"),
        P("dp", "kv", "head"),
        P(),
    )
    out_specs = (P("dp", "head", "kv"), P("head"))
    return jax.shard_map(
        per_device, mesh=mesh, in_specs=in_specs, out_specs=out_specs, check_vma=False
    )
```

profile of v0, /device:TPU:0, one launch (start us, length us, event | category | flops | bytes accessed | tf_op | source)
XLA Modules:
  0.0 131.6 jit_solution(168695083922571773)
XLA Ops:
  7.2 0.0 copy-start
  7.2 0.0 copy-start.1
  7.2 0.0 copy-start.2
  7.2 0.0 all-gather.5.cloned.1.call-start
  7.2 2.3 %copy.18 = bf16[1,256,1792]{1,2,0:T(8,128)(2,1)} copy(bf16[1,256,1792]{2,1,0:T(8,128)(2,1)} %param.7) | data formatting | bytes 1835008 | tf_op args[0]
  9.5 0.0 all-gather.5.cloned.1.call-update
  9.5 0.0 all-gather.3.cloned.1.call-start
  9.6 1.0 copy.17
  10.6 7.2 %all_gather.12 = bf16[1,256,512]{1,2,0:T(8,128)(2,1)} all-gather(bf16[1,256,256]{1,2,0:T(8,128)(2,1)S(1)} %copy.17), channel_id=1, replica_groups=mesh['dp'=4,'head'=2,'kv'=4] {'head'}, dimensions={2}, use_global_device_ids=true | all-gather | bytes 393216 | tf_op jit(solution)/shard_map/all_gather | solution.py:114
  17.8 0.0 all-gather.3.cloned.1.call-update
  17.9 0.6 slice.3
  20.1 0.0 copy-done
  20.1 0.1 constant_dynamic-slice_fusion.1
  20.2 0.1 copy.16
  20.2 0.1 reshape.172
  20.3 0.1 reshape.174
  21.0 0.0 copy-done.1
  21.0 0.2 copy.21
  21.2 0.3 copy.22
  21.5 0.0 copy-done.2
  21.5 14.4 %all_gather.15 = bf16[1,1024,128]{2,1,0:T(8,128)(2,1)S(1)} all-gather(bf16[1,256,128]{2,1,0:T(8,128)(2,1)S(1)} %copy-done.2), channel_id=1, replica_groups=mesh['dp'=4,'head'=2,'kv'=4] {'kv'}, dimensions={1}, use_global_device_ids=true | all-gather | bytes 327680 | tf_op jit(solution)/shard_map/all_gather | solution.py:131
  35.9 6.6 %all-gather.5.cloned.1.call-done = bf16[1,256,3584]{1,2,0:T(8,128)(2,1)} async-done(((bf16[1,256,1792]{1,2,0:T(8,128)(2,1)}), bf16[1,256,3584]{1,2,0:T(8,128)(2,1)}) %all-gather.5.cloned.1.call-update) | async-done | bytes 1835024 | tf_op jit(solution)/shard_map/all_gather | solution.py:113
  42.5 2.9 %copy.20 = bf16[256,28,128]{2,0,1:T(8,128)(2,1)S(1)} copy(bf16[256,28,128]{0,2,1:T(8,128)(2,1)} %bitcast.99) | data formatting | bytes 3670016 | tf_op jit(solution)/shard_map/reshape | solution.py:119
  45.4 0.7 gather_fusion.1
  46.2 1.1 bitcast_select_fusion.1
  47.3 26.8 %all-gather.3.cloned.1.call-done = bf16[1,1024,512]{1,2,0:T(8,128)(2,1)} async-done(((bf16[1,256,512]{1,2,0:T(8,128)(2,1)}), bf16[1,1024,512]{1,2,0:T(8,128)(2,1)}) %all-gather.3.cloned.1.call-update) | async-done | bytes 1048592 | tf_op jit(solution)/shard_map/all_gather | solution.py:130
  74.1 9.4 %while.19 = (s32[]{:T(128)}, f32[1,14,256]{2,1,0:T(8,128)S(1)}, f32[1,14,256]{2,1,0:T(8,128)S(1)}, f32[1,14,256]{2,1,0:T(8,128)S(1)}, f32[1,7,256]{2,1,0:T(8,128...) while((s32[]{:T(128)}, f32[1,14,256]{2,1,0:T(8,128)S(1)}, ...), condition=%wide.region_6.7_spmd.clone, body=%wide.region_0.6_spmd.clone.sunk | while | flops 732774400 | bytes 36064820 | solution.py:74
  74.1 1.1 constant_dynamic-slice_fusion.3
  75.2 0.3 copy.24
  75.5 0.9 gather_fusion
  76.4 0.1 broadcast_compare_fusion.2
  76.6 2.6 %fusion.28 = (f32[14,256]{1,0:T(8,128)S(1)}, f32[14,512,256]{2,1,0:T(8,128)S(1)}) fusion(pred[256,512]{0,1:T(8,128)(4,1)S(1)} %broadcast_compare_fusion.2, bf16[1,256,14,128]{3,1,2,0:T(8,128)(2,1)} %get-tuple-element.346, bf16[14,512,128]{2,1,0:T(8,128)(2,1)S(1)} %gather_fusion, pred[14]{0:T(512)(128)(4,1)S(1)} %compare_and_fusion.5), kind=kOutput, calls=%fused_computation.9.clone.1 | convolution fusion | flops 476180992 | bytes 10237966 | tf_op jit(solution)/shard_map/while/body/bqpd,bkpd->bpqk/dot_general | solution.py:48
  79.3 0.8 select_reduce_fusion.4
  80.1 2.6 %fusion.29 = (f32[14,256]{1,0:T(8,128)S(1)}, f32[14,256]{1,0:T(8,128)S(1)}) fusion(f32[14,512,256]{2,1,0:T(8,128)S(1)} %get-tuple-element.292, f32[7,256,512]{1,2,0:T(8,128)S(1)} %get-tuple-element.293, f32[14,256]{1,0:T(8,128)S(1)} %bitcast.97, pred[256,512]{0,1:T(8,128)(4,1)S(1)} %broadcast_compare_fusion.2), kind=kLoop, calls=%fused_computation.6.clone.1 | loop fusion | flops 14672896 | bytes 11184128 | tf_op jit(solution)/shard_map/while/body/reduce_sum | solution.py:71
  82.7 0.8 select_reduce_fusion.5
  83.6 0.1 fusion.23
  83.7 0.1 reduce_sum.63
  83.8 0.1 reduce_sum.64
  83.9 0.6 reduce_sum.61
  84.5 39.7 %psum.7 = f32[7]{0:T(128)S(1)} all-reduce(f32[7]{0:T(128)S(1)} %reduce_sum.64), channel_id=1, replica_groups=mesh['dp'=4,'head'=2,'kv'=4] {'dp','kv'}, use_global_device_ids=true, to_apply=%region_10.11 | all-reduce | flops 7 | bytes 56 | tf_op jit(solution)/shard_map/psum | solution.py:138
  124.3 0.5 broadcast_multiply_fusion
  (28 shorter events, 0.2 us)
Async XLA Ops:
  7.2 12.9 %copy-start = (s32[14,2]{0,1:T(2,128)S(1)}, s32[14,2]{0,1:T(2,128)}, u32[]{:S(2)}) copy-start(s32[14,2]{0,1:T(2,128)} %param.11) | copy-start | bytes 340
  7.2 13.8 %copy-start.1 = (bf16[1,256,896]{2,1,0:T(8,128)(2,1)S(1)}, bf16[1,256,896]{2,1,0:T(8,128)(2,1)}, u32[]{:S(2)}) copy-start(bf16[1,256,896]{2,1,0:T(8,128)(2,1)} %param.9) | copy-start | bytes 1376260
  7.2 14.3 %copy-start.2 = (bf16[1,256,128]{2,1,0:T(8,128)(2,1)S(1)}, bf16[1,256,128]{2,1,0:T(8,128)(2,1)}, u32[]{:S(2)}) copy-start(bf16[1,256,128]{2,1,0:T(8,128)(2,1)} %param.10) | copy-start | bytes 196612
  7.2 35.3 %all-gather.5.cloned.1.call-start = ((), (), s32[]{:S(2)}) async-start(), calls=%async_computation.1 | async-start | bytes 2752512 | tf_op jit(solution)/shard_map/all_gather | solution.py:113
  9.5 64.5 %all-gather.3.cloned.1.call-start = ((), (), s32[]{:S(2)}) async-start(), calls=%async_computation | async-start | bytes 1310720 | tf_op jit(solution)/shard_map/all_gather | solution.py:130
Sparse Core Ops, SparseCore 0:
  9.7 32.8 all-gather.4
  44.1 29.9 all-gather.2
where the time goes:
time: 132 us
  blocking collectives  61.4 us (47%)
  waiting for transfers between devices  33.5 us (25%)
  between operations  16.4 us (12%)
  local copies, waits for them, and re-layouts  11.3 us (9%)
  other arithmetic  5.49 us (4%)
  matrix products  3.37 us (3%)
    psum x1, blocking collectives, per_device(): total = lax.psum(head_sums, ('dp', 'kv'))  39.7 us
    all_gather x1, waiting for transfers between devices, per_device(): lax.all_gather(all_tk, 'kv', axis=1, tiled=True)  26.8 us
    all_gather x1, blocking collectives, per_device(): lax.all_gather(student_key, 'kv', axis=1, tiled=True)  14.4 us
    all_gather x1, blocking collectives, per_device(): lax.all_gather(teacher_key, 'head', axis=2, tiled=True)  7.22 us
    all_gather x1, waiting for transfers between devices, per_device(): lax.all_gather(teacher_query, 'head', axis=2, tiled=True)  6.6 us
    unnamed x10, local copies, waits for them, and re-layouts  3.76 us
    reshape x1, local copies, waits for them, and re-layouts, per_device(): all_tq.reshape(seq_dev, row_count, HT, DH)  2.89 us
  transfers between devices with their start and end apart: 2, of which 2 were waited for; matrix products, arithmetic and copies ran while one was open for 5% of the time, Pallas kernels for 0%

commit v1 on v0

--- a/solution.py
+++ b/solution.py
@@ -111,7 +111,7 @@
     query_pos = kv_index * row_count + jnp.arange(row_count, dtype=jnp.int32)
     all_tq, all_tk = (
         lax.all_gather(teacher_query, "head", axis=2, tiled=True),
-        lax.all_gather(teacher_key, "head", axis=2, tiled=True),
+        jnp.concatenate(lax.all_gather(teacher_key, "head"), axis=2),
     )
     my_pairs = lax.dynamic_slice_in_dim(
         pair_table, head_index * local_student, local_student, 0

time: 132 us -> 132 us (level)
    unnamed x10 -> x9, local copies, waits for them, and re-layouts: 3.76 us -> 2.76 us
where the time goes in v1:
time: 132 us
  blocking collectives  61.5 us (47%)
  waiting for transfers between devices  33.5 us (25%)
  between operations  16.4 us (12%)
  local copies, waits for them, and re-layouts  11.1 us (8%)
  other arithmetic  5.49 us (4%)
  matrix products  3.37 us (3%)
    psum x1, blocking collectives, per_device(): total = lax.psum(head_sums, ('dp', 'kv'))  39.7 us
    all_gather x1, waiting for transfers between devices, per_device(): lax.all_gather(all_tk, 'kv', axis=1, tiled=True)  26.8 us
    all_gather x1, blocking collectives, per_device(): lax.all_gather(student_key, 'kv', axis=1, tiled=True)  14.3 us
    all_gather x1, blocking collectives, per_device(): lax.all_gather(teacher_key, 'head')  7.39 us
    all_gather x1, waiting for transfers between devices, per_device(): lax.all_gather(teacher_query, 'head', axis=2, tiled=True)  6.68 us
    reshape x1, local copies, waits for them, and re-layouts, per_device(): all_tq.reshape(seq_dev, row_count, HT, DH)  2.89 us
    unnamed x9, local copies, waits for them, and re-layouts  2.76 us
  transfers between devices with their start and end apart: 2, of which 2 were waited for; matrix products, arithmetic and copies ran while one was open for 5% of the time, Pallas kernels for 0%

profile of v1, /device:TPU:0, one launch (start us, length us, event | category | flops | bytes accessed | tf_op | source)
XLA Modules:
  0.0 131.6 jit_solution(8342393406558869494)
XLA Ops:
  7.2 0.0 copy-start
  7.2 0.0 copy-start.1
  7.2 0.0 copy-start.2
  7.2 0.0 all-gather.6.cloned.1.call-start
  7.2 2.3 %copy.35 = bf16[1,256,1792]{1,2,0:T(8,128)(2,1)} copy(bf16[1,256,1792]{2,1,0:T(8,128)(2,1)} %param.7) | data formatting | bytes 1835008 | tf_op args[0]
  9.5 0.0 all-gather.6.cloned.1.call-update
  9.5 0.0 all-gather.4.cloned.1.call-start
  9.6 7.4 %all-gather = bf16[2,256,256]{2,1,0:T(8,128)(2,1)S(1)} all-gather(bf16[1,256,256]{2,1,0:T(8,128)(2,1)} %param.8), channel_id=2, replica_groups=mesh['dp'=4,'head'=2,'kv'=4] {'head'}, dimensions={0}, use_global_device_ids=true | all-gather | bytes 393216 | tf_op jit(solution)/shard_map/all_gather | solution.py:114
  17.0 0.8 copy.34
  17.8 0.0 all-gather.4.cloned.1.call-update
  17.8 0.6 slice.3
  20.1 0.0 copy-done
  20.1 0.1 constant_dynamic-slice_fusion.1
  20.1 0.1 copy.33
  20.2 0.1 reshape.178
  20.3 0.1 reshape.182
  21.0 0.0 copy-done.1
  21.0 0.2 copy.38
  21.2 0.3 copy.39
  21.5 0.0 copy-done.2
  21.5 14.3 %all_gather.19 = bf16[1,1024,128]{2,1,0:T(8,128)(2,1)S(1)} all-gather(bf16[1,256,128]{2,1,0:T(8,128)(2,1)S(1)} %copy-done.2), channel_id=1, replica_groups=mesh['dp'=4,'head'=2,'kv'=4] {'kv'}, dimensions={1}, use_global_device_ids=true | all-gather | bytes 327680 | tf_op jit(solution)/shard_map/all_gather | solution.py:131
  35.9 6.7 %all-gather.6.cloned.1.call-done = bf16[1,256,3584]{1,2,0:T(8,128)(2,1)} async-done(((bf16[1,256,1792]{1,2,0:T(8,128)(2,1)}), bf16[1,256,3584]{1,2,0:T(8,128)(2,1)}) %all-gather.6.cloned.1.call-update) | async-done | bytes 1835024 | tf_op jit(solution)/shard_map/all_gather | solution.py:113
  42.5 2.9 %copy.37 = bf16[256,28,128]{2,0,1:T(8,128)(2,1)S(1)} copy(bf16[256,28,128]{0,2,1:T(8,128)(2,1)} %bitcast.104) | data formatting | bytes 3670016 | tf_op jit(solution)/shard_map/reshape | solution.py:119
  45.4 0.7 gather_fusion.1
  46.2 1.1 bitcast_select_fusion.1
  47.3 26.8 %all-gather.4.cloned.1.call-done = bf16[1,1024,512]{1,2,0:T(8,128)(2,1)} async-done(((bf16[1,256,512]{1,2,0:T(8,128)(2,1)}), bf16[1,1024,512]{1,2,0:T(8,128)(2,1)}) %all-gather.4.cloned.1.call-update) | async-done | bytes 1048592 | tf_op jit(solution)/shard_map/all_gather | solution.py:130
  74.1 9.4 %while.19 = (s32[]{:T(128)}, f32[1,14,256]{2,1,0:T(8,128)S(1)}, f32[1,14,256]{2,1,0:T(8,128)S(1)}, f32[1,14,256]{2,1,0:T(8,128)S(1)}, f32[1,7,256]{2,1,0:T(8,128...) while((s32[]{:T(128)}, f32[1,14,256]{2,1,0:T(8,128)S(1)}, ...), condition=%wide.region_6.7_spmd.clone, body=%wide.region_0.6_spmd.clone.sunk | while | flops 732774400 | bytes 36064820 | solution.py:74
  74.1 1.1 constant_dynamic-slice_fusion.3
  75.2 0.3 copy.41
  75.5 0.9 gather_fusion
  76.4 0.1 broadcast_compare_fusion.2
  76.6 2.6 %fusion.28 = (f32[14,256]{1,0:T(8,128)S(1)}, f32[14,512,256]{2,1,0:T(8,128)S(1)}) fusion(pred[256,512]{0,1:T(8,128)(4,1)S(1)} %broadcast_compare_fusion.2, bf16[1,256,14,128]{3,1,2,0:T(8,128)(2,1)} %get-tuple-element.376, bf16[14,512,128]{2,1,0:T(8,128)(2,1)S(1)} %gather_fusion, pred[14]{0:T(512)(128)(4,1)S(1)} %compare_and_fusion.5), kind=kOutput, calls=%fused_computation.9.clone.1 | convolution fusion | flops 476180992 | bytes 10237966 | tf_op jit(solution)/shard_map/while/body/bqpd,bkpd->bpqk/dot_general | solution.py:48
  79.3 0.8 select_reduce_fusion.4
  80.1 2.6 %fusion.29 = (f32[14,256]{1,0:T(8,128)S(1)}, f32[14,256]{1,0:T(8,128)S(1)}) fusion(f32[14,512,256]{2,1,0:T(8,128)S(1)} %get-tuple-element.322, f32[7,256,512]{1,2,0:T(8,128)S(1)} %get-tuple-element.323, f32[14,256]{1,0:T(8,128)S(1)} %bitcast.102, pred[256,512]{0,1:T(8,128)(4,1)S(1)} %broadcast_compare_fusion.2), kind=kLoop, calls=%fused_computation.6.clone.1 | loop fusion | flops 14672896 | bytes 11184128 | tf_op jit(solution)/shard_map/while/body/reduce_sum | solution.py:71
  82.7 0.8 select_reduce_fusion.5
  83.6 0.1 fusion.23
  83.7 0.1 reduce_sum.63
  83.8 0.1 reduce_sum.64
  83.9 0.6 reduce_sum.61
  84.5 39.7 %psum.7 = f32[7]{0:T(128)S(1)} all-reduce(f32[7]{0:T(128)S(1)} %reduce_sum.64), channel_id=1, replica_groups=mesh['dp'=4,'head'=2,'kv'=4] {'dp','kv'}, use_global_device_ids=true, to_apply=%region_10.11 | all-reduce | flops 7 | bytes 56 | tf_op jit(solution)/shard_map/psum | solution.py:138
  124.3 0.5 broadcast_multiply_fusion
  (28 shorter events, 0.2 us)
Async XLA Ops:
  7.2 12.9 %copy-start = (s32[14,2]{0,1:T(2,128)S(1)}, s32[14,2]{0,1:T(2,128)}, u32[]{:S(2)}) copy-start(s32[14,2]{0,1:T(2,128)} %param.11) | copy-start | bytes 340
  7.2 13.8 %copy-start.1 = (bf16[1,256,896]{2,1,0:T(8,128)(2,1)S(1)}, bf16[1,256,896]{2,1,0:T(8,128)(2,1)}, u32[]{:S(2)}) copy-start(bf16[1,256,896]{2,1,0:T(8,128)(2,1)} %param.9) | copy-start | bytes 1376260
  7.2 14.3 %copy-start.2 = (bf16[1,256,128]{2,1,0:T(8,128)(2,1)S(1)}, bf16[1,256,128]{2,1,0:T(8,128)(2,1)}, u32[]{:S(2)}) copy-start(bf16[1,256,128]{2,1,0:T(8,128)(2,1)} %param.10) | copy-start | bytes 196612
  7.2 35.3 %all-gather.6.cloned.1.call-start = ((), (), s32[]{:S(2)}) async-start(), calls=%async_computation.1 | async-start | bytes 2752512 | tf_op jit(solution)/shard_map/all_gather | solution.py:113
  9.5 64.5 %all-gather.4.cloned.1.call-start = ((), (), s32[]{:S(2)}) async-start(), calls=%async_computation | async-start | bytes 1310720 | tf_op jit(solution)/shard_map/all_gather | solution.py:130
Sparse Core Ops, SparseCore 0:
  9.7 32.8 all-gather.5
  44.1 29.9 all-gather.3
